TPU v7x, 32 devices: a whole 2x2x4 slice. The times are simulated.
32 devices in a mesh: dp: 8 (over y, x, core), mp: 4 (over z).
Axes of the slice: x: 2, y: 2, z: 4, core: 2. Of those that a mesh axis runs over, the one named last changes fastest.
Arguments:
- tokens: bfloat16 [8192, 2048], P('dp'), may hold values from -6 to 6
- cotangent: bfloat16 [8192, 2048], P('dp'), may hold values from -6 to 6
- counts: int32 [8], replicated, may hold values from 1 to 1024, 5120 in all
- w_qkv: bfloat16 [2048, 3, 2048], P('dp', None, 'mp'), may hold values from -0.125 to 0.125
- w_out: bfloat16 [2048, 2048], P('mp', 'dp'), may hold values from -1 to 1
- w_fc1: bfloat16 [2048, 8192], P('dp', 'mp'), may hold values from -0.125 to 0.125
- w_fc2: bfloat16 [8192, 2048], P('mp', 'dp'), may hold values from -0.0625 to 0.0625
- ln1_gain: bfloat16 [2048], P('dp'), may hold values from 0.5 to 1.5
- ln1_bias: bfloat16 [2048], P('dp'), may hold values from -1.796875 to 1.796875
- ln2_gain: bfloat16 [2048], P('dp'), may hold values from 0.5 to 1.5
- ln2_bias: bfloat16 [2048], P('dp'), may hold values from -1.796875 to 1.796875
- qv_bias: bfloat16 [2, 2048], P(None, ('mp', 'dp')), may hold values from -1.796875 to 1.796875
- out_bias: bfloat16 [2048], P('dp'), may hold values from -1.796875 to 1.796875
- fc1_bias: bfloat16 [8192], P(('mp', 'dp')), may hold values from -1.796875 to 1.796875
- fc2_bias: bfloat16 [2048], P('dp'), may hold values from -1.796875 to 1.796875
Outputs:
- out_tokens: bfloat16 [8192, 2048], P('dp')
- grad_tokens: float32 [8192, 2048], P('dp')
- grad_w_qkv: float32 [2048, 3, 2048], P('dp', None, 'mp')
- grad_w_out: float32 [2048, 2048], P('mp', 'dp')
- grad_w_fc1: float32 [2048, 8192], P('dp', 'mp')
- grad_w_fc2: float32 [8192, 2048], P('mp', 'dp')
- grad_ln1_gain: float32 [2048], P('dp')
- grad_ln1_bias: float32 [2048], P('dp')
- grad_ln2_gain: float32 [2048], P('dp')
- grad_ln2_bias: float32 [2048], P('dp')
- grad_qv_bias: float32 [2, 2048], P(None, ('mp', 'dp'))
- grad_out_bias: float32 [2048], P('dp')
- grad_fc1_bias: float32 [8192], P(('mp', 'dp'))
- grad_fc2_bias: float32 [2048], P('dp')
Inputs may be any that keep to these rules, and one draw needn't show every extreme that they name: counts[g] is the number of live tokens of group g's sequence, at the start of its 1024 slots; the largest count equals 1024.
All inputs are finite; a program needn't handle non-finite values.
Results may differ from a plain program's by a relative error of at most 0.014.
Values may be sent and summed in bfloat16 or wider, within the bound.
A program may use at most 192 MiB of HBM per device.

v0:
```python
import math
import jax
import jax.numpy as jnp
from jax import lax
from jax.sharding import PartitionSpec as P

HEAD = 128
EPS = 1e-05
NEG = -1e30


def layer_norm(values, gain_vec, shift_vec):
    center = values - jnp.mean(values, axis=-1, keepdims=True)
    spread = jnp.mean(center * center, axis=-1, keepdims=True)
    return center * lax.rsqrt(spread + EPS) * gain_vec + shift_vec


def smooth_gate(values):
    return jax.nn.gelu(values, approximate=True)


def causal_scores(queries, key_heads, inv_root):
    row_count = queries.shape[0]
    raw_scores = (
        jnp.einsum("qhd,khd->hqk", queries, key_heads, preferred_element_type=jnp.float32)
        * inv_root
    )
    future = lax.broadcasted_iota(jnp.int32, (row_count, row_count), 1) > lax.broadcasted_iota(
        jnp.int32, (row_count, row_count), 0
    )
    return jnp.where(future[None], NEG, raw_scores)


def shards(
    tokens,
    cotangent,
    counts,
    w_qkv,
    w_out,
    w_fc1,
    w_fc2,
    ln1_gain,
    ln1_bias,
    ln2_gain,
    ln2_bias,
    qv_bias,
    out_bias,
    fc1_bias,
    fc2_bias,
):
    gathered = (
        lax.all_gather(w_qkv, "dp", axis=0, tiled=True),
        lax.all_gather(w_out, "dp", axis=1, tiled=True),
        lax.all_gather(w_fc1, "dp", axis=0, tiled=True),
        lax.all_gather(w_fc2, "dp", axis=1, tiled=True),
        lax.all_gather(ln1_gain, "dp", axis=0, tiled=True),
        lax.all_gather(ln1_bias, "dp", axis=0, tiled=True),
        lax.all_gather(ln2_gain, "dp", axis=0, tiled=True),
        lax.all_gather(ln2_bias, "dp", axis=0, tiled=True),
        lax.all_gather(qv_bias, "dp", axis=1, tiled=True),
        lax.all_gather(out_bias, "dp", axis=0, tiled=True),
        lax.all_gather(fc1_bias, "dp", axis=0, tiled=True),
        lax.all_gather(fc2_bias, "dp", axis=0, tiled=True),
    )
    whole_qkv, whole_out, whole_fc1, whole_fc2 = (
        gathered[0],
        gathered[1],
        gathered[2],
        gathered[3],
    )
    gain_one = gathered[4].astype(jnp.float32)
    shift_one = gathered[5].astype(jnp.float32)
    gain_two = gathered[6].astype(jnp.float32)
    shift_two = gathered[7].astype(jnp.float32)
    bias_qv = gathered[8].astype(jnp.float32)
    bias_out = gathered[9].astype(jnp.float32)
    bias_fc1 = gathered[10].astype(jnp.float32)
    bias_fc2 = gathered[11].astype(jnp.float32)
    seq_rows = tokens.shape[0]
    local_width = whole_qkv.shape[2]
    heads_here = local_width // HEAD
    inv_root = 1.0 / math.sqrt(HEAD)
    inputs = tokens.astype(jnp.float32)
    normed_one = layer_norm(inputs, gain_one, shift_one).astype(jnp.bfloat16)
    projected = jnp.einsum("sd,dce->sce", normed_one, whole_qkv, preferred_element_type=jnp.float32)
    queries = (
        (projected[:, 0] + bias_qv[0]).astype(jnp.bfloat16).reshape(seq_rows, heads_here, HEAD)
    )
    key_heads = projected[:, 1].astype(jnp.bfloat16).reshape(seq_rows, heads_here, HEAD)
    values = (projected[:, 2] + bias_qv[1]).astype(jnp.bfloat16).reshape(seq_rows, heads_here, HEAD)
    scores = causal_scores(queries, key_heads, inv_root)
    row_peak = jnp.max(scores, axis=-1, keepdims=True)
    exp_terms = jnp.exp(scores - row_peak)
    exp_total = jnp.sum(exp_terms, axis=-1, keepdims=True)
    log_total = row_peak + jnp.log(exp_total)
    prob_low = (exp_terms / exp_total).astype(jnp.bfloat16)
    mixed_heads = (
        jnp.einsum("hqk,khd->qhd", prob_low, values, preferred_element_type=jnp.float32)
        .astype(jnp.bfloat16)
        .reshape(seq_rows, local_width)
    )
    attn_part = jnp.dot(mixed_heads, whole_out, preferred_element_type=jnp.float32)
    residual = inputs + lax.psum(attn_part, "mp") + bias_out
    normed_two = layer_norm(residual, gain_two, shift_two).astype(jnp.bfloat16)
    preact = jnp.dot(normed_two, whole_fc1, preferred_element_type=jnp.float32) + bias_fc1
    activated = smooth_gate(preact).astype(jnp.bfloat16)
    ffn_part = jnp.dot(activated, whole_fc2, preferred_element_type=jnp.float32)
    out_tokens = (
        residual + lax.psum(ffn_part.astype(jnp.bfloat16), "mp").astype(jnp.float32) + bias_fc2
    ).astype(jnp.bfloat16)
    dp_index = lax.axis_index("dp")
    slot_ids = lax.iota(jnp.int32, counts.shape[0])
    own_count = jnp.sum(jnp.where(slot_ids == dp_index, counts, 0))
    weight_share = own_count.astype(jnp.float32) / jnp.sum(counts).astype(jnp.float32)
    live_rows = lax.iota(jnp.int32, seq_rows) < own_count
    grad_out = jnp.where(live_rows[:, None], cotangent.astype(jnp.float32), 0.0)
    grad_out_low = grad_out.astype(jnp.bfloat16)
    grad_fc2 = (
        jnp.einsum("sf,sd->fd", activated, grad_out_low, preferred_element_type=jnp.float32)
        * weight_share
    )
    grad_fc2_bias = jnp.sum(grad_out, axis=0) * weight_share
    delta_act = jnp.einsum("sd,fd->sf", grad_out_low, whole_fc2, preferred_element_type=jnp.float32)
    unused_gate, gate_back = jax.vjp(smooth_gate, preact)
    delta_pre = gate_back(delta_act)[0]
    grad_fc1_bias = jnp.sum(delta_pre, axis=0) * weight_share
    delta_pre_low = delta_pre.astype(jnp.bfloat16)
    grad_fc1 = (
        jnp.einsum("sd,sf->df", normed_two, delta_pre_low, preferred_element_type=jnp.float32)
        * weight_share
    )
    two_part = jnp.einsum("sf,df->sd", delta_pre_low, whole_fc1, preferred_element_type=jnp.float32)
    delta_two = lax.psum(two_part, "mp")
    unused_two, second_back = jax.vjp(layer_norm, residual, gain_two, shift_two)
    resid_part, gain_two_part, shift_two_part = second_back(delta_two)
    delta_resid = resid_part + grad_out
    delta_resid_low = delta_resid.astype(jnp.bfloat16)
    out_bias_part = jnp.sum(delta_resid, axis=0)
    grad_out_proj = (
        jnp.einsum("sc,sd->cd", mixed_heads, delta_resid_low, preferred_element_type=jnp.float32)
        * weight_share
    )
    delta_mixed = jnp.einsum(
        "sd,cd->sc", delta_resid_low, whole_out, preferred_element_type=jnp.float32
    )
    delta_mixed_low = delta_mixed.astype(jnp.bfloat16).reshape(seq_rows, heads_here, HEAD)
    scores_again = causal_scores(queries, key_heads, inv_root)
    prob_full = jnp.exp(scores_again - log_total)
    delta_prob = jnp.einsum(
        "qhd,khd->hqk", delta_mixed_low, values, preferred_element_type=jnp.float32
    )
    delta_scores = prob_full * (
        delta_prob - jnp.sum(prob_full * delta_prob, axis=-1, keepdims=True)
    )
    delta_scores_low = delta_scores.astype(jnp.bfloat16)
    delta_q = (
        jnp.einsum("hqk,khd->qhd", delta_scores_low, key_heads, preferred_element_type=jnp.float32)
        * inv_root
    ).reshape(seq_rows, local_width)
    delta_k = (
        jnp.einsum("hqk,qhd->khd", delta_scores_low, queries, preferred_element_type=jnp.float32)
        * inv_root
    ).reshape(seq_rows, local_width)
    delta_v = jnp.einsum(
        "hqk,qhd->khd", prob_low, delta_mixed_low, preferred_element_type=jnp.float32
    ).reshape(seq_rows, local_width)
    grad_qv = jnp.stack([jnp.sum(delta_q, axis=0), jnp.sum(delta_v, axis=0)]) * weight_share
    delta_proj = jnp.stack([delta_q, delta_k, delta_v], axis=1).astype(jnp.bfloat16)
    grad_qkv = (
        jnp.einsum("sd,sce->dce", normed_one, delta_proj, preferred_element_type=jnp.float32)
        * weight_share
    )
    one_part = jnp.einsum("sce,dce->sd", delta_proj, whole_qkv, preferred_element_type=jnp.float32)
    delta_one = lax.psum(one_part.astype(jnp.bfloat16), "mp").astype(jnp.float32)
    unused_one, first_back = jax.vjp(layer_norm, inputs, gain_one, shift_one)
    input_part, gain_one_part, shift_one_part = first_back(delta_one)
    grad_tokens = input_part + delta_resid
    stat_sums = jnp.stack(
        [gain_two_part, shift_two_part, out_bias_part, gain_one_part, shift_one_part]
    )
    stat_weighted = stat_sums * weight_share
    summed_all = (
        lax.psum_scatter(grad_qkv, "dp", scatter_dimension=0, tiled=True),
        lax.psum_scatter(grad_out_proj, "dp", scatter_dimension=1, tiled=True),
        lax.psum_scatter(grad_qv, "dp", scatter_dimension=1, tiled=True),
        lax.psum_scatter(stat_weighted[2], "dp", scatter_dimension=0, tiled=True),
        lax.psum_scatter(stat_weighted[3], "dp", scatter_dimension=0, tiled=True),
        lax.psum_scatter(stat_weighted[4], "dp", scatter_dimension=0, tiled=True),
        lax.psum_scatter(grad_fc1, "dp", scatter_dimension=0, tiled=True),
        lax.psum_scatter(grad_fc2, "dp", scatter_dimension=1, tiled=True),
        lax.psum_scatter(grad_fc1_bias, "dp", scatter_dimension=0, tiled=True),
        lax.psum_scatter(grad_fc2_bias, "dp", scatter_dimension=0, tiled=True),
        lax.psum_scatter(stat_weighted[0], "dp", scatter_dimension=0, tiled=True),
        lax.psum_scatter(stat_weighted[1], "dp", scatter_dimension=0, tiled=True),
    )
    return (
        out_tokens,
        grad_tokens,
        summed_all[0],
        summed_all[1],
        summed_all[6],
        summed_all[7],
        summed_all[4],
        summed_all[5],
        summed_all[10],
        summed_all[11],
        summed_all[2],
        summed_all[3],
        summed_all[8],
        summed_all[9],
    )


def solution(mesh):
    placed = (
        P("dp", None),
        P("dp", None),
        P(),
        P("dp", None, "mp"),
        P("mp", "dp"),
        P("dp", "mp"),
        P("mp", "dp"),
        P("dp"),
        P("dp"),
        P("dp"),
        P("dp"),
        P(None, ("mp", "dp")),
        P("dp"),
        P(("mp", "dp")),
        P("dp"),
    )
    return jax.shard_map(
        shards,
        mesh=mesh,
        in_specs=placed,
        out_specs=(
            P("dp", None),
            P("dp", None),
            P("dp", None, "mp"),
            P("mp", "dp"),
            P("dp", "mp"),
            P("mp", "dp"),
            P("dp"),
            P("dp"),
            P("dp"),
            P("dp"),
            P(None, ("mp", "dp")),
            P("dp"),
            P(("mp", "dp")),
            P("dp"),
        ),
        check_vma=False,
    )
```

profile of v0, /device:TPU:0, one launch (start us, length us, event | category | flops | bytes accessed | tf_op | source)
XLA Modules:
  0.0 1627.1 jit_solution(16595095688366546610)
XLA Ops:
  12.0 10.4 all-gather.2
  46.3 13.5 all-gather.13.cloned.1.call-done
  59.8 10.4 fusion.38
  147.5 254.6 %all-reduce.13.cloned.1.call-done = f32[1024,2048]{1,0:T(8,128)} async-done(((f32[1024,2048]{1,0:T(8,128)}), f32[1024,2048]{1,0:T(8,128)}) %all-reduce.13.cloned.1.call-update) | async-done | bytes 8388624 | tf_op jit(solution)/shard_map/psum | solution.py:103
  412.4 44.7 %all-gather.17.cloned.1.call-done = bf16[2048,2048]{1,0:T(8,128)(2,1)} async-done(((bf16[256,2048]{1,0:T(8,128)(2,1)}), bf16[2048,2048]{1,0:T(8,128)(2,1)}) %all-gather.17.cloned.1.call-update) | async-done | bytes 8388624 | tf_op jit(solution)/shard_map/all_gather | solution.py:54
  457.1 16.0 fusion.48
  473.1 41.7 %all-gather.19.cloned.1.call-done = bf16[2048,2048]{1,0:T(8,128)(2,1)} async-done(((bf16[2048,256]{1,0:T(8,128)(2,1)}), bf16[2048,2048]{1,0:T(8,128)(2,1)}) %all-gather.19.cloned.1.call-update) | async-done | bytes 8388624 | tf_op jit(solution)/shard_map/all_gather | solution.py:55
  514.7 20.5 %fusion.58 = (f32[2048]{0:T(1024)}, bf16[1024,2048]{1,0:T(8,128)(2,1)S(1)}) fusion(f32[1024,2048]{1,0:T(8,128)} %fusion.48, f32[2048]{0:T(1024)S(1)} %bitcast.123, bf16[2048,2048]{1,0:T(8,128)(2,1)} %all-gather.19.cloned.1.call-done, bf16[1024,2048]{1,0:T(8,128)(2,1)} %param.16, pred[1024]{0:T(1024)(128)(4,1)S(1)} %iota_compare_fusion.1), kind=kOutput, calls=%fused_computation.107 | convolution fusion | flops 8642361344 | bytes 25183232 | tf_op jit(solution)/shard_map/sd,fd->sf/dot_general | solution.py:123
  537.2 13.2 fusion.27
  551.9 16.9 %convolution_convert_fusion = bf16[1024,2048]{1,0:T(8,128)(2,1)} fusion(bf16[2048,2048]{1,0:T(8,128)(2,1)} %all-gather.19.cloned.1.call-done, f32[1024,2048]{1,0:T(8,128)} %fusion.48, f32[2048]{0:T(1024)S(1)} %bitcast.124), kind=kOutput, calls=%fused_computation.53 | convolution fusion | flops 8613003264 | bytes 20979712 | tf_op jit(solution)/shard_map/dot_general | solution.py:107
  568.8 272.7 %all-reduce.15.cloned.1.call-done = f32[1024,2048]{1,0:T(8,128)} async-done(((f32[1024,2048]{1,0:T(8,128)}), f32[1024,2048]{1,0:T(8,128)}) %all-reduce.15.cloned.1.call-update) | async-done | bytes 8388624 | tf_op jit(solution)/shard_map/psum | solution.py:133
  864.3 10.6 multiply_reduce_fusion
  874.9 12.4 multiply_convert_fusion
  902.1 11.0 bitcast_convert_fusion
  914.3 9.2 convolution_multiply_fusion.2
  923.6 17.6 %convolution_multiply_fusion = f32[2048,2048]{1,0:T(8,128)} fusion(f32[]{:T(128)S(6)} %div.63, bf16[1024,2048]{1,0:T(8,128)(2,1)} %param.16, pred[1024]{0:T(1024)(128)(4,1)S(1)} %iota_compare_fusion.1, f32[1024,2048]{1,0:T(8,128)} %fusion.48, f32[2048]{0:T(1024)S(1)} %bitcast.125), kind=kOutput, calls=%fused_computation.23 | convolution fusion | flops 8621391872 | bytes 29369348 | tf_op jit(solution)/shard_map/sf,sd->fd/dot_general | solution.py:119
  941.9 17.1 %convolution_multiply_fusion.1 = f32[2048,2048]{1,0:T(8,128)} fusion(f32[]{:T(128)S(6)} %div.63, bf16[1024,2048]{1,0:T(8,128)(2,1)} %copy-done.43, f32[1024,2048]{1,0:T(8,128)} %copy-done, f32[2048]{0:T(1024)S(1)} %bitcast.122, f32[2048]{0:T(1024)S(1)} %bitcast.98, f32[1024]{0:T(1024)S(1)} %fusion.42, f32[1024]{0:T(1024)S(1)} %broadcast_multiply_fusion.4), kind=kOutput, calls=%fused_computation.24 | convolution fusion | flops 8604614656 | bytes 29384708 | tf_op jit(solution)/shard_map/sd,sf->df/dot_general | solution.py:129
  960.3 13.7 broadcast_multiply_fusion
  986.2 242.6 %all-reduce.17.cloned.1.call-done = (bf16[1024,2048]{1,0:T(8,128)(2,1)}, bf16[1024,2048]{1,0:T(8,128)(2,1)}) async-done(((bf16[1024,2048]{1,0:T(8,128)(2,1)}, bf16[1024,2048]{1,0:T(8,128)(2,1)}), (bf16[1024,2048]{1,0:T(8,128)(2,1)}, bf16[1024,2048]{1,0:T(8,128)(2,1)})) %all-reduce.17.cloned.1.call-update) | async-done | bytes 8388624 | tf_op jit(solution)/shard_map/psum | solution.py:109
  1239.3 10.4 fusion.19
  1249.8 25.4 %all-reduce.7 = (f32[2048]{0:T(1024)S(1)}, f32[2048]{0:T(1024)S(1)}, f32[2048]{0:T(1024)S(1)}, f32[2048]{0:T(1024)S(1)}, f32[2048]{0:T(1024)S(1)}, /*index=5*/f32[2048]{0:T(1024)S(1)}, f32[2048]{0:T(1024)S(1)}) all-reduce(f32[2048]{0:T(1024)S(1)} %bitcast.111, f32[2048]{0:T(1024)S(1)} %bitcast.110, ...), channel_id=6, replica_groups=mesh['dp'=8,'mp'=4] {'dp'}, use_global_device_ids=true, to_apply=%region_26.27.clone | all-reduce | flops 14336 | bytes 114688
  1288.2 115.5 %reduce-scatter.14.cloned.1.call-done = f32[2048,256]{1,0:T(8,128)} async-done(((f32[2048,2048]{1,0:T(8,128)}), f32[2048,256]{1,0:T(8,128)}) %reduce-scatter.14.cloned.1.call-update) | async-done | bytes 2097168 | tf_op jit(solution)/shard_map/reduce_scatter | solution.py:190
  1403.7 120.4 %reduce-scatter.12.cloned.1.call-done = f32[256,2048]{1,0:T(8,128)} async-done(((f32[2048,2048]{1,0:T(8,128)}), f32[256,2048]{1,0:T(8,128)}) %reduce-scatter.12.cloned.1.call-update) | async-done | bytes 2097168 | tf_op jit(solution)/shard_map/reduce_scatter | solution.py:189
  1524.0 96.0 %reduce-scatter.8.cloned.1.call-done = f32[256,3,512]{2,0,1:T(8,128)} async-done(((f32[2048,3,512]{2,0,1:T(8,128)}), f32[256,3,512]{2,0,1:T(8,128)}) %reduce-scatter.8.cloned.1.call-update) | async-done | bytes 1572880 | tf_op jit(solution)/shard_map/reduce_scatter | solution.py:183
  (199 shorter events, 193.5 us)
Async XLA Ops:
  7.2 52.6 %all-gather.13.cloned.1.call-start = ((), (), s32[]{:S(2)}) async-start(), calls=%async_computation.5 | async-start | bytes 7077888 | tf_op jit(solution)/shard_map/all_gather | solution.py:52
  9.5 93.5 %all-gather.15.cloned.1.call-start = ((), (), s32[]{:S(2)}) async-start(), calls=%async_computation.6 | async-start | bytes 2359296 | tf_op jit(solution)/shard_map/all_gather | solution.py:53
  10.3 391.8 %all-reduce.13.cloned.1.call-start = ((), (), s32[]{:S(2)}) async-start(), calls=%async_computation.7 | async-start | bytes 16777216 | tf_op jit(solution)/shard_map/psum | solution.py:103
  22.4 49.7 %copy-start.29 = (f32[1,512]{1,0:T(1,128)}, f32[1,512]{1,0:T(1,128)S(1)}, u32[]{:S(2)}) copy-start(f32[1,512]{1,0:T(1,128)S(1)} %get-tuple-element.47) | copy-start | bytes 6148
  25.3 44.9 %copy-start.21 = (f32[1024]{0:T(1024)}, f32[1024]{0:T(1024)S(1)}, u32[]{:S(2)}) copy-start(f32[1024]{0:T(1024)S(1)} %broadcast_multiply_fusion.5) | copy-start | bytes 12292
  28.8 41.5 %copy-start.23 = (f32[1024]{0:T(1024)}, f32[1024]{0:T(1024)S(1)}, u32[]{:S(2)}) copy-start(f32[1024]{0:T(1024)S(1)} %fusion.41) | copy-start | bytes 12292
  37.7 32.6 %copy-start.31 = (f32[8,1,256]{2,1,0:T(1,128)}, f32[8,1,256]{2,1,0:T(1,128)S(1)}, u32[]{:S(2)}) copy-start(f32[8,1,256]{2,1,0:T(1,128)S(1)} %convert_element_type.130) | copy-start | bytes 24580
  46.3 23.9 %copy-start.19 = (f32[8,1,256]{2,1,0:T(1,128)}, f32[8,1,256]{2,1,0:T(1,128)S(1)}, u32[]{:S(2)}) copy-start(f32[8,1,256]{2,1,0:T(1,128)S(1)} %convert_element_type.129) | copy-start | bytes 24580
  110.8 35.4 %copy-start.36 = (s32[8]{0:T(128)S(1)}, s32[8]{0:T(128)}, u32[]{:S(2)}) copy-start(s32[8]{0:T(128)} %param.17) | copy-start | bytes 100
  110.9 346.2 %all-gather.17.cloned.1.call-start = ((), (), s32[]{:S(2)}) async-start(), calls=%async_computation.8 | async-start | bytes 9437184 | tf_op jit(solution)/shard_map/all_gather | solution.py:54
  111.5 403.3 %all-gather.19.cloned.1.call-start = ((), (), s32[]{:S(2)}) async-start(), calls=%async_computation.9 | async-start | bytes 9437184 | tf_op jit(solution)/shard_map/all_gather | solution.py:55
  112.0 729.4 %all-reduce.15.cloned.1.call-start = ((), (), s32[]{:S(2)}) async-start(), calls=%async_computation.10 | async-start | bytes 16777216 | tf_op jit(solution)/shard_map/psum | solution.py:133
  138.2 318.9 %copy-start.34 = (f32[8,1,256]{2,1,0:T(1,128)}, f32[8,1,256]{2,1,0:T(1,128)S(1)}, u32[]{:S(2)}) copy-start(f32[8,1,256]{2,1,0:T(1,128)S(1)} %convert_element_type.134) | copy-start | bytes 24580
  550.5 434.4 %reduce-scatter.16.cloned.1.call-start = ((), (), s32[]{:S(2)}) async-start(), calls=%async_computation.15 | async-start | bytes 294912
  849.7 11.7 slice-start
  874.9 12.4 copy-start.7
  874.9 12.4 copy-start.30
  902.0 326.9 %all-reduce.17.cloned.1.call-start = ((), (), s32[]{:S(2)}) async-start(), calls=%async_computation.16 | async-start | bytes 16777216 | tf_op jit(solution)/shard_map/psum | solution.py:109
  913.1 375.1 %reduce-scatter.10.cloned.1.call-start = ((), (), s32[]{:S(2)}) async-start(), calls=%async_computation.12 | async-start | bytes 4718592 | tf_op jit(solution)/shard_map/reduce_scatter | solution.py:184
  923.5 480.1 %reduce-scatter.14.cloned.1.call-start = ((), (), s32[]{:S(2)}) async-start(), calls=%async_computation.14 | async-start | bytes 18874368 | tf_op jit(solution)/shard_map/reduce_scatter | solution.py:190
  941.2 582.8 %reduce-scatter.12.cloned.1.call-start = ((), (), s32[]{:S(2)}) async-start(), calls=%async_computation.13 | async-start | bytes 18874368 | tf_op jit(solution)/shard_map/reduce_scatter | solution.py:189
  959.0 661.0 %reduce-scatter.8.cloned.1.call-start = ((), (), s32[]{:S(2)}) async-start(), calls=%async_computation.11 | async-start | bytes 14155776 | tf_op jit(solution)/shard_map/reduce_scatter | solution.py:183
  974.0 10.8 copy-start.33
  974.0 260.5 %copy-start.26 = (f32[1024]{0:T(1024)S(1)}, f32[1024]{0:T(1024)}, u32[]{:S(2)}) copy-start(f32[1024]{0:T(1024)} %copy-done.25) | copy-start | bytes 12292
  (34 other events, 160.4 us)
Sparse Core Ops, SparseCore 0:
  10.4 49.3 all-gather.12
  61.7 28.0 all-gather.14
  111.0 291.0 all-reduce.12
  403.8 53.2 all-gather.16
  458.8 55.8 all-gather.18
  550.6 290.8 all-reduce.14
  902.1 32.6 reduce-scatter.15
  938.0 290.8 all-reduce.16
  1232.8 50.8 reduce-scatter.9
  1287.7 115.9 reduce-scatter.13
  1407.8 116.1 reduce-scatter.11
  1527.9 92.0 reduce-scatter.7
where the time goes:
time: 1630 us
  waiting for transfers between devices  1200 us (74%)
  matrix products  190 us (12%)
  blocking collectives  96.2 us (6%)
  other arithmetic  87.9 us (5%)
  local copies, waits for them, and re-layouts  32.2 us (2%)
  between operations  17.2 us (1%)
    psum x1, waiting for transfers between devices, shards(): delta_two = lax.psum(two_part, 'mp')  273 us
    psum x1, waiting for transfers between devices, shards(): residual = inputs + lax.psum(attn_part, 'mp') + bias_out  255 us
    psum x1, waiting for transfers between devices, shards(): lax.psum(ffn_part.astype(jnp.bfloat16), 'mp').astype(jnp.float32)  243 us
    reduce_scatter x1, waiting for transfers between devices, shards(): lax.psum_scatter(grad_fc1, 'dp', scatter_dimension=0, tiled=True)  120 us
    reduce_scatter x1, waiting for transfers between devices, shards(): lax.psum_scatter(grad_fc2, 'dp', scatter_dimension=1, tiled=True)  115 us
    reduce_scatter x1, waiting for transfers between devices, shards(): lax.psum_scatter(grad_qkv, 'dp', scatter_dimension=0, tiled=True)  96 us
    all_gather x1, waiting for transfers between devices, shards(): lax.all_gather(w_fc1, 'dp', axis=0, tiled=True)  44.7 us
    all_gather x1, waiting for transfers between devices, shards(): lax.all_gather(w_fc2, 'dp', axis=1, tiled=True)  41.7 us
  transfers between devices with their start and end apart: 12, of which 9 were waited for; matrix products, arithmetic and copies ran while one was open for 12% of the time, Pallas kernels for 0%

commit v1 on v0

--- a/solution.py
+++ b/solution.py
@@ -130,7 +130,11 @@
         * weight_share
     )
     two_part = jnp.einsum("sf,df->sd", delta_pre_low, whole_fc1, preferred_element_type=jnp.float32)
-    delta_two = lax.psum(two_part, "mp")
+    delta_two = two_part
+    for hop in (1, 2):
+        delta_two = delta_two + lax.ppermute(
+            delta_two, "mp", [(dev, dev ^ hop) for dev in range(4)]
+        )
     unused_two, second_back = jax.vjp(layer_norm, residual, gain_two, shift_two)
     resid_part, gain_two_part, shift_two_part = second_back(delta_two)
     delta_resid = resid_part + grad_out

time: 1630 us -> 1900 us (1.17)
  waiting for transfers between devices: 1200 us -> 1460 us
    ppermute x0 -> x2, waiting for transfers between devices: none -> 524 us  [shards(): lax.ppermute(delta_two, 'mp', [(dev, dev ^ hop) for dev in range(4)])]
    psum x1 -> x0, waiting for transfers between devices: 273 us -> none  [shards(): delta_two = lax.psum(two_part, 'mp')]
  transfers between devices with their start and end apart: 12 -> 13, of which waited for: 9 -> 10; matrix products, arithmetic and copies ran while one was open for 12% -> 10% of each run, Pallas kernels for 0% -> 0%
where the time goes in v1:
time: 1900 us
  waiting for transfers between devices  1460 us (77%)
  matrix products  188 us (10%)
  other arithmetic  99 us (5%)
  blocking collectives  96.5 us (5%)
  local copies, waits for them, and re-layouts  35.1 us (2%)
    ppermute x2, waiting for transfers between devices, shards(): lax.ppermute(delta_two, 'mp', [(dev, dev ^ hop) for dev in range(4)])  524 us
    psum x1, waiting for transfers between devices, shards(): residual = inputs + lax.psum(attn_part, 'mp') + bias_out  255 us
    psum x1, waiting for transfers between devices, shards(): lax.psum(ffn_part.astype(jnp.bfloat16), 'mp').astype(jnp.float32)  245 us
    reduce_scatter x1, waiting for transfers between devices, shards(): lax.psum_scatter(grad_fc2, 'dp', scatter_dimension=1, tiled=True)  120 us
    reduce_scatter x1, waiting for transfers between devices, shards(): lax.psum_scatter(grad_fc1, 'dp', scatter_dimension=0, tiled=True)  116 us
    reduce_scatter x1, waiting for transfers between devices, shards(): lax.psum_scatter(grad_qkv, 'dp', scatter_dimension=0, tiled=True)  96.2 us
    all_gather x1, waiting for transfers between devices, shards(): lax.all_gather(w_fc1, 'dp', axis=0, tiled=True)  44.7 us
    all_gather x1, waiting for transfers between devices, shards(): lax.all_gather(w_fc2, 'dp', axis=1, tiled=True)  41.6 us
  transfers between devices with their start and end apart: 13, of which 10 were waited for; matrix products, arithmetic and copies ran while one was open for 10% of the time, Pallas kernels for 0%

profile of v1, /device:TPU:0, one launch (start us, length us, event | category | flops | bytes accessed | tf_op | source)
XLA Modules:
  0.0 1895.7 jit_solution(18335797854649424697)
XLA Ops:
  11.3 10.4 all-gather.1
  47.2 12.6 all-gather.13.cloned.1.call-done
  59.8 10.4 fusion.38
  147.2 254.5 %all-reduce.12.cloned.1.call-done = f32[1024,2048]{1,0:T(8,128)} async-done(((f32[1024,2048]{1,0:T(8,128)}), f32[1024,2048]{1,0:T(8,128)}) %all-reduce.12.cloned.1.call-update) | async-done | bytes 8388624 | tf_op jit(solution)/shard_map/psum | solution.py:103
  412.0 44.7 %all-gather.17.cloned.1.call-done = bf16[2048,2048]{1,0:T(8,128)(2,1)} async-done(((bf16[256,2048]{1,0:T(8,128)(2,1)}), bf16[2048,2048]{1,0:T(8,128)(2,1)}) %all-gather.17.cloned.1.call-update) | async-done | bytes 8388624 | tf_op jit(solution)/shard_map/all_gather | solution.py:54
  456.8 16.0 fusion.48
  472.8 41.6 %all-gather.19.cloned.1.call-done = bf16[2048,2048]{1,0:T(8,128)(2,1)} async-done(((bf16[2048,256]{1,0:T(8,128)(2,1)}), bf16[2048,2048]{1,0:T(8,128)(2,1)}) %all-gather.19.cloned.1.call-update) | async-done | bytes 8388624 | tf_op jit(solution)/shard_map/all_gather | solution.py:55
  514.4 20.5 %fusion.58 = (f32[2048]{0:T(1024)}, bf16[1024,2048]{1,0:T(8,128)(2,1)S(1)}) fusion(f32[1024,2048]{1,0:T(8,128)} %fusion.48, f32[2048]{0:T(1024)S(1)} %bitcast.121, bf16[2048,2048]{1,0:T(8,128)(2,1)} %all-gather.19.cloned.1.call-done, bf16[1024,2048]{1,0:T(8,128)(2,1)} %param.16, pred[1024]{0:T(1024)(128)(4,1)S(1)} %iota_compare_fusion.1), kind=kOutput, calls=%fused_computation.107 | convolution fusion | flops 8642361344 | bytes 25183232 | tf_op jit(solution)/shard_map/sd,fd->sf/dot_general | solution.py:123
  534.9 12.8 fusion.27
  552.4 181.2 %collective-permute-done = f32[1024,2048]{1,0:T(8,128)} collective-permute-done((f32[1024,2048]{1,0:T(8,128)S(1)}, f32[1024,2048]{1,0:T(8,128)}, u32[]{:S(2)}, u32[]{:S(2)}) %collective-permute-start) | collective-permute-done | bytes 8388640 | tf_op jit(solution)/shard_map/ppermute | solution.py:135
  733.6 11.7 add.172
  749.1 16.1 convolution_convert_fusion
  765.2 342.8 %collective-permute-done.1 = f32[1024,2048]{1,0:T(8,128)} collective-permute-done((f32[1024,2048]{1,0:T(8,128)}, f32[1024,2048]{1,0:T(8,128)}, u32[]{:S(2)}, u32[]{:S(2)}) %collective-permute-start.1) | collective-permute-done | bytes 8388640 | tf_op jit(solution)/shard_map/ppermute | solution.py:135
  1131.3 10.6 multiply_reduce_fusion
  1141.9 12.1 multiply_convert_fusion
  1169.9 11.0 bitcast_convert_fusion
  1191.3 16.4 convolution_multiply_fusion.1
  1207.8 17.8 convolution_multiply_fusion
  1227.2 13.6 broadcast_multiply_fusion
  1253.0 244.7 %all-reduce.14.cloned.1.call-done = (bf16[1024,2048]{1,0:T(8,128)(2,1)}, bf16[1024,2048]{1,0:T(8,128)(2,1)}) async-done(((bf16[1024,2048]{1,0:T(8,128)(2,1)}, bf16[1024,2048]{1,0:T(8,128)(2,1)}), (bf16[1024,2048]{1,0:T(8,128)(2,1)}, bf16[1024,2048]{1,0:T(8,128)(2,1)})) %all-reduce.14.cloned.1.call-update) | async-done | bytes 8388624 | tf_op jit(solution)/shard_map/psum | solution.py:109
  1518.6 25.5 %all-reduce.7 = (f32[2048]{0:T(1024)S(1)}, f32[2048]{0:T(1024)S(1)}, f32[2048]{0:T(1024)S(1)}, f32[2048]{0:T(1024)S(1)}, f32[2048]{0:T(1024)S(1)}, /*index=5*/f32[2048]{0:T(1024)S(1)}, f32[2048]{0:T(1024)S(1)}) all-reduce(f32[2048]{0:T(1024)S(1)} %bitcast.111, f32[2048]{0:T(1024)S(1)} %bitcast.110, ...), channel_id=6, replica_groups=mesh['dp'=8,'mp'=4] {'dp'}, use_global_device_ids=true, to_apply=%region_25.26.clone | all-reduce | flops 14336 | bytes 114688
  1556.9 115.9 %reduce-scatter.12.cloned.1.call-done = f32[256,2048]{1,0:T(8,128)} async-done(((f32[2048,2048]{1,0:T(8,128)}), f32[256,2048]{1,0:T(8,128)}) %reduce-scatter.12.cloned.1.call-update) | async-done | bytes 2097168 | tf_op jit(solution)/shard_map/reduce_scatter | solution.py:193
  1672.8 120.0 %reduce-scatter.14.cloned.1.call-done = f32[2048,256]{1,0:T(8,128)} async-done(((f32[2048,2048]{1,0:T(8,128)}), f32[2048,256]{1,0:T(8,128)}) %reduce-scatter.14.cloned.1.call-update) | async-done | bytes 2097168 | tf_op jit(solution)/shard_map/reduce_scatter | solution.py:194
  1792.8 96.2 %reduce-scatter.8.cloned.1.call-done = f32[256,3,512]{2,0,1:T(8,128)} async-done(((f32[2048,3,512]{2,0,1:T(8,128)}), f32[256,3,512]{2,0,1:T(8,128)}) %reduce-scatter.8.cloned.1.call-update) | async-done | bytes 1572880 | tf_op jit(solution)/shard_map/reduce_scatter | solution.py:187
  (205 shorter events, 219.8 us)
Async XLA Ops:
  7.2 31.3 %copy-start.37 = (bf16[2,64]{1,0:T(2,128)(2,1)S(1)}, bf16[2,64]{1,0:T(2,128)(2,1)}, u32[]{:S(2)}) copy-start(bf16[2,64]{1,0:T(2,128)(2,1)} %param.26) | copy-start | bytes 772
  7.2 52.6 %all-gather.13.cloned.1.call-start = ((), (), s32[]{:S(2)}) async-start(), calls=%async_computation.5 | async-start | bytes 7077888 | tf_op jit(solution)/shard_map/all_gather | solution.py:52
  9.5 93.2 %all-gather.15.cloned.1.call-start = ((), (), s32[]{:S(2)}) async-start(), calls=%async_computation.6 | async-start | bytes 2359296 | tf_op jit(solution)/shard_map/all_gather | solution.py:53
  10.3 391.5 %all-reduce.12.cloned.1.call-start = ((), (), s32[]{:S(2)}) async-start(), calls=%async_computation.7 | async-start | bytes 16777216 | tf_op jit(solution)/shard_map/psum | solution.py:103
  21.7 48.6 %copy-start.32 = (f32[8,1,256]{2,1,0:T(1,128)}, f32[8,1,256]{2,1,0:T(1,128)S(1)}, u32[]{:S(2)}) copy-start(f32[8,1,256]{2,1,0:T(1,128)S(1)} %convert_element_type.130) | copy-start | bytes 24580
  31.6 38.7 %copy-start.20 = (f32[8,1,256]{2,1,0:T(1,128)}, f32[8,1,256]{2,1,0:T(1,128)S(1)}, u32[]{:S(2)}) copy-start(f32[8,1,256]{2,1,0:T(1,128)S(1)} %convert_element_type.129) | copy-start | bytes 24580
  34.5 35.9 %copy-start.22 = (f32[1024]{0:T(1024)}, f32[1024]{0:T(1024)S(1)}, u32[]{:S(2)}) copy-start(f32[1024]{0:T(1024)S(1)} %broadcast_multiply_fusion.5) | copy-start | bytes 12292
  38.5 31.8 %copy-start.24 = (f32[1024]{0:T(1024)}, f32[1024]{0:T(1024)S(1)}, u32[]{:S(2)}) copy-start(f32[1024]{0:T(1024)S(1)} %fusion.41) | copy-start | bytes 12292
  47.2 25.0 %copy-start.30 = (f32[1,512]{1,0:T(1,128)}, f32[1,512]{1,0:T(1,128)S(1)}, u32[]{:S(2)}) copy-start(f32[1,512]{1,0:T(1,128)S(1)} %get-tuple-element.48) | copy-start | bytes 6148
  110.5 27.3 %copy-start.42 = (bf16[256]{0:T(256)(128)(2,1)S(1)}, bf16[256]{0:T(256)(128)(2,1)}, u32[]{:S(2)}) copy-start(bf16[256]{0:T(256)(128)(2,1)} %param.28) | copy-start | bytes 1540
  110.5 35.4 %copy-start.38 = (s32[8]{0:T(128)S(1)}, s32[8]{0:T(128)}, u32[]{:S(2)}) copy-start(s32[8]{0:T(128)} %param.17) | copy-start | bytes 100
  110.6 346.2 %all-gather.17.cloned.1.call-start = ((), (), s32[]{:S(2)}) async-start(), calls=%async_computation.8 | async-start | bytes 9437184 | tf_op jit(solution)/shard_map/all_gather | solution.py:54
  111.2 403.2 %all-gather.19.cloned.1.call-start = ((), (), s32[]{:S(2)}) async-start(), calls=%async_computation.9 | async-start | bytes 9437184 | tf_op jit(solution)/shard_map/all_gather | solution.py:55
  111.7 1139.9 %reduce-scatter.16.cloned.1.call-start = ((), (), s32[]{:S(2)}) async-start(), calls=%async_computation.14 | async-start | bytes 294912
  129.0 327.8 %copy-start.35 = (f32[8,1,256]{2,1,0:T(1,128)}, f32[8,1,256]{2,1,0:T(1,128)S(1)}, u32[]{:S(2)}) copy-start(f32[8,1,256]{2,1,0:T(1,128)S(1)} %convert_element_type.134) | copy-start | bytes 24580
  550.9 182.7 %collective-permute-start = (f32[1024,2048]{1,0:T(8,128)S(1)}, f32[1024,2048]{1,0:T(8,128)}, u32[]{:S(2)}, u32[]{:S(2)}) collective-permute-start(f32[1024,2048]{1,0:T(8,128)S(1)} %fusion.27), channel_id=1, source_target_pairs={{0,1},{1,0},{2,3},{3,2},{4,5},{5,4},{6,7},{7,6},{8,9},{9,8},{10,11... | collective-permute-start | bytes 25165832 | tf_op jit(solution)/shard_map/ppermute | solution.py:135
  745.3 362.7 %collective-permute-start.1 = (f32[1024,2048]{1,0:T(8,128)}, f32[1024,2048]{1,0:T(8,128)}, u32[]{:S(2)}, u32[]{:S(2)}) collective-permute-start(f32[1024,2048]{1,0:T(8,128)} %add.172), channel_id=1, source_target_pairs={{0,2},{1,3},{2,0},{3,1},{4,6},{5,7},{6,4},{7,5},{8,10},{9,11},{10,... | collective-permute-start | bytes 25165832 | tf_op jit(solution)/shard_map/ppermute | solution.py:135
  749.1 359.0 %copy-start.5 = (f32[1024,2048]{1,0:T(8,128)S(1)}, f32[1024,2048]{1,0:T(8,128)}, u32[]{:S(2)}) copy-start(f32[1024,2048]{1,0:T(8,128)} %add.172) | copy-start | bytes 25165828
  1169.8 327.8 %all-reduce.14.cloned.1.call-start = ((), (), s32[]{:S(2)}) async-start(), calls=%async_computation.15 | async-start | bytes 16777216 | tf_op jit(solution)/shard_map/psum | solution.py:109
  1180.9 376.1 %reduce-scatter.10.cloned.1.call-start = ((), (), s32[]{:S(2)}) async-start(), calls=%async_computation.11 | async-start | bytes 4718592 | tf_op jit(solution)/shard_map/reduce_scatter | solution.py:188
  1191.3 481.5 %reduce-scatter.12.cloned.1.call-start = ((), (), s32[]{:S(2)}) async-start(), calls=%async_computation.12 | async-start | bytes 18874368 | tf_op jit(solution)/shard_map/reduce_scatter | solution.py:193
  1207.8 585.1 %reduce-scatter.14.cloned.1.call-start = ((), (), s32[]{:S(2)}) async-start(), calls=%async_computation.13 | async-start | bytes 18874368 | tf_op jit(solution)/shard_map/reduce_scatter | solution.py:194
  1225.7 663.3 %reduce-scatter.8.cloned.1.call-start = ((), (), s32[]{:S(2)}) async-start(), calls=%async_computation.10 | async-start | bytes 14155776 | tf_op jit(solution)/shard_map/reduce_scatter | solution.py:187
  1240.7 262.5 %copy-start.27 = (f32[1024]{0:T(1024)S(1)}, f32[1024]{0:T(1024)}, u32[]{:S(2)}) copy-start(f32[1024]{0:T(1024)} %copy-done.26) | copy-start | bytes 12292
  (37 other events, 239.9 us)
Sparse Core Ops, SparseCore 0:
  10.4 49.3 all-gather.12
  61.7 28.0 all-gather.14
  110.7 291.0 all-reduce.11
  403.5 53.2 all-gather.16
  458.5 55.8 all-gather.18
  1169.9 33.6 reduce-scatter.15
  1206.8 290.8 all-reduce.13
  1501.6 50.8 reduce-scatter.9
  1556.6 116.1 reduce-scatter.11
  1676.8 115.9 reduce-scatter.13
  1796.9 92.0 reduce-scatter.7
